TPU v7x, 32 devices: a whole 2x2x4 slice. The times are simulated.
32 devices in a mesh: gx: 4 (over y, x), gy: 2 (over core), gz: 4 (over z).
Axes of the slice: x: 2, y: 2, z: 4, core: 2. Of those that a mesh axis runs over, the one named last changes fastest.
Arguments:
- positions: float32 [3, 8, 8, 8, 128], P(None, 'gx', 'gy', 'gz'), may hold values from 0 to 1
- type_ids: int32 [8, 8, 8, 128], P('gx', 'gy', 'gz'), may hold values from 0 to 1
- counts: int32 [8, 8, 8], P('gx', 'gy', 'gz'), may hold values from 64 to 128
- type_charge: float32 [2], replicated, may hold values from -1 to 1
- type_sigma: float32 [2], replicated, may hold values from 0.2 to 0.35
- type_epsilon: float32 [2], replicated, may hold values from 0.05 to 0.5
Outputs:
- forces: float32 [3, 8, 8, 8, 128], P(None, 'gx', 'gy', 'gz')
- totals: float32 [2], replicated
All inputs are finite; a program needn't handle non-finite values.
Results may differ from a plain program's by a relative error of at most 0.0003.
Values sent between devices are 32-bit elements; how exact they have to be, the bound alone decides.
A program may use at most 64 MiB of HBM per device.

v0:
```python
import jax
import jax.numpy as jnp
from jax import lax
from jax.sharding import PartitionSpec as P

soft_core = 0.09
corner_pairs = [
    (first_corner, second_corner)
    for first_corner in range(8)
    for second_corner in range(8)
    if first_corner & second_corner == 0 and first_corner <= second_corner
]


def passed_along(value, axis, steps):
    count = lax.axis_size(axis)
    pairs = [(source, (source + steps) % count) for source in range(count)]
    return lax.ppermute(value, axis, pairs)


def corner_of(which):
    return (which & 1, which >> 1 & 1, which >> 2 & 1)


def atom_table(positions, type_ids, counts, type_charge, type_sigma, type_epsilon):
    type_count = type_charge.shape[0]
    kinds_shape = (type_count, 1, 1, 1, 1)
    onehot = (
        type_ids[None] == jnp.arange(type_count, dtype=jnp.int32).reshape(kinds_shape)
    ).astype(jnp.float32)
    charge = jnp.sum(onehot * type_charge.reshape(kinds_shape), 0)
    sigma_atom = jnp.sum(onehot * type_sigma.reshape(kinds_shape), 0)
    depth_atom = jnp.sum(onehot * jnp.sqrt(type_epsilon).reshape(kinds_shape), 0)
    slots = lax.broadcasted_iota(jnp.int32, type_ids.shape, 3)
    occupied = (slots < counts[..., None]).astype(jnp.float32)
    return jnp.stack(
        [positions[0], positions[1], positions[2], charge, sigma_atom, depth_atom, occupied]
    )


def pair_terms(first, second, offset, selfpair):
    displace = second[:3, :, None, :] - first[:3, :, :, None] + offset[:, None, None, None]
    dist_sq = jnp.sum(displace * displace, 0)
    width_atoms = first.shape[-1]
    live_mask = first[6][:, :, None] * second[6][:, None, :] * (dist_sq < 1.0).astype(jnp.float32)
    if selfpair:
        ordered = (
            lax.broadcasted_iota(jnp.int32, (width_atoms, width_atoms), 0)
            < lax.broadcasted_iota(jnp.int32, (width_atoms, width_atoms), 1)
        ).astype(jnp.float32)
        live_mask = live_mask * ordered[None]
    sigma_pair = 0.5 * (first[4][:, :, None] + second[4][:, None, :])
    depth_pair = first[5][:, :, None] * second[5][:, None, :]
    coulomb = first[3][:, :, None] * second[3][:, None, :]
    soft_sq = dist_sq + soft_core
    inverse = lax.rsqrt(soft_sq)
    ratio_six = (sigma_pair * sigma_pair / soft_sq) ** 3
    ratio_twelve = ratio_six * ratio_six
    value_here = 4.0 * depth_pair * (ratio_twelve - ratio_six) + coulomb * inverse
    slope_here = (
        4.0 * depth_pair * (6.0 * ratio_six - 12.0 * ratio_twelve) - coulomb * inverse
    ) * inverse
    cut_sq = 1.0 + soft_core
    cut_len = cut_sq**0.5
    cut_six = (sigma_pair * sigma_pair / cut_sq) ** 3
    cut_twelve = cut_six * cut_six
    value_cut = 4.0 * depth_pair * (cut_twelve - cut_six) + coulomb / cut_len
    slope_cut = (
        4.0 * depth_pair * (6.0 * cut_six - 12.0 * cut_twelve) - coulomb / cut_len
    ) / cut_len
    energy = live_mask * (value_here - value_cut - (soft_sq * inverse - cut_len) * slope_cut)
    slope = live_mask * (slope_here - slope_cut) * inverse
    weighted = slope[None] * displace
    return (jnp.sum(weighted, 3), -jnp.sum(weighted, 2), jnp.sum(energy), jnp.sum(slope * dist_sq))


def per_device(positions, type_ids, counts, type_charge, type_sigma, type_epsilon):
    features = atom_table(positions, type_ids, counts, type_charge, type_sigma, type_epsilon)
    size_x, size_y, size_z, width_atoms = features.shape[1:]
    extended = jnp.concatenate([features, passed_along(features[:, :1], "gx", -1)], 1)
    extended = jnp.concatenate([extended, passed_along(extended[:, :, :1], "gy", -1)], 2)
    extended = jnp.concatenate([extended, passed_along(extended[:, :, :, :1], "gz", -1)], 3)
    cell_rows = size_x * size_y * size_z

    def slabs_of(which):
        shift_x, shift_y, shift_z = corner_of(which)
        view = extended[
            :, shift_x : shift_x + size_x, shift_y : shift_y + size_y, shift_z : shift_z + size_z
        ]
        return view.reshape((7, cell_rows, width_atoms))

    reaction = jnp.zeros((3, size_x + 1, size_y + 1, size_z + 1, width_atoms), jnp.float32)

    def deposit(reaction, force_rows, which):
        shift_x, shift_y, shift_z = corner_of(which)
        grid = force_rows.reshape((3, size_x, size_y, size_z, width_atoms))
        return reaction.at[
            :, shift_x : shift_x + size_x, shift_y : shift_y + size_y, shift_z : shift_z + size_z
        ].add(grid)

    energy = jnp.float32(0.0)
    virial = jnp.float32(0.0)
    for first_corner, second_corner in corner_pairs:
        offset = jnp.array(
            [float(a - b) for a, b in zip(corner_of(second_corner), corner_of(first_corner))],
            jnp.float32,
        )
        selfpair = first_corner == second_corner
        force_first, force_second, energies, virials = pair_terms(
            slabs_of(first_corner), slabs_of(second_corner), offset, selfpair
        )
        reaction = deposit(reaction, force_first, first_corner)
        reaction = deposit(reaction, force_second, second_corner)
        energy = energy + energies
        virial = virial + virials
    returned = passed_along(reaction[:, :, :, size_z:], "gz", 1)
    reaction = reaction[:, :, :, :size_z].at[:, :, :, :1].add(returned)
    returned = passed_along(reaction[:, :, size_y:], "gy", 1)
    reaction = reaction[:, :, :size_y].at[:, :, :1].add(returned)
    returned = passed_along(reaction[:, size_x:], "gx", 1)
    forces = reaction[:, :size_x].at[:, :1].add(returned)
    summed = lax.psum((energy, virial), ("gx", "gy", "gz"))
    normaliser = 1.0 / (
        size_x
        * lax.axis_size("gx")
        * size_y
        * lax.axis_size("gy")
        * size_z
        * lax.axis_size("gz")
        * width_atoms
    )
    totals = jnp.stack([summed[0], summed[1]]) * normaliser
    return (forces, totals)


def solution(mesh):
    in_specs = (
        P(None, "gx", "gy", "gz", None),
        P("gx", "gy", "gz", None),
        P("gx", "gy", "gz"),
        P(),
        P(),
        P(),
    )
    out_specs = (P(None, "gx", "gy", "gz", None), P())
    return jax.shard_map(
        per_device, mesh=mesh, in_specs=in_specs, out_specs=out_specs, check_vma=False
    )
```

profile of v0, /device:TPU:0, one launch (start us, length us, event | category | flops | bytes accessed | tf_op | source)
XLA Modules:
  0.0 161.4 jit_solution(2301316743114900686)
XLA Ops:
  0.6 0.0 copy-start.5
  0.6 0.0 copy-start.13
  0.7 0.0 copy-start.14
  0.7 0.0 copy-start.6
  0.7 0.0 copy-start.15
  0.7 0.0 copy-start
  0.7 0.7 copy.33
  1.4 0.7 sqrt.3
  2.1 0.7 constant_dynamic-update-slice_fusion.4
  2.8 0.8 copy.32
  3.6 0.8 select_reduce_fusion.2
  4.4 0.1 constant_dynamic-update-slice_fusion
  4.5 4.0 %collective-permute-start = (f32[7,1,4,2,128]{4,3,2,1,0:T(2,128)S(1)}, f32[7,1,4,2,128]{4,3,2,1,0:T(2,128)S(1)}, u32[]{:S(2)}, u32[]{:S(2)}) collective-permute-start(f32[7,1,4,2,128]{4,3,2,1,0:T(2,128)S(1)} %slice.1661), channel_id=1, source_target_pairs={{0,24},{8,0},{16,8},{24,16},{1,25},{9,1},{17,9},{25,17},{2,26},{10... | collective-permute-start | bytes 86024 | tf_op jit(solution)/shard_map/ppermute | solution.py:18
  8.5 0.1 lt.135
  8.6 0.1 fusion.332
  8.7 1.3 collective-permute-done
  10.1 0.1 collective-permute-start.1
  10.2 1.2 collective-permute-done.1
  11.4 3.7 %collective-permute-start.2 = (f32[7,3,5,1,128]{4,3,2,1,0:T(1,128)S(1)}, f32[7,3,5,1,128]{4,3,2,1,0:T(1,128)S(1)}, u32[]{:S(2)}, u32[]{:S(2)}) collective-permute-start(f32[7,3,5,1,128]{4,3,2,1,0:T(1,128)S(1)} %slice.1680), channel_id=1, source_target_pairs={{0,3},{1,0},{2,1},{3,2},{4,7},{5,4},{6,5},{7,6},{8,11},{9,8},{10,9... | collective-permute-start | bytes 161288 | tf_op jit(solution)/shard_map/ppermute | solution.py:18
  15.1 1.8 %collective-permute-done.2 = f32[7,3,5,1,128]{4,3,2,1,0:T(1,128)S(1)} collective-permute-done((f32[7,3,5,1,128]{4,3,2,1,0:T(1,128)S(1)}, f32[7,3,5,1,128]{4,3,2,1,0:T(1,128)S(1)}, u32[]{:S(2)}, u32[]{:S(2)}) %collective-permute-start.2) | collective-permute-done | bytes 53792 | tf_op jit(solution)/shard_map/ppermute | solution.py:18
  16.9 0.1 pad_maximum_fusion
  17.1 3.5 %multiply_reduce_fusion.1 = (f32[16,128,128]{2,1,0:T(8,128)S(1)}, f32[16,128,128]{2,1,0:T(8,128)S(1)}, f32[16,128,128]{2,1,0:T(8,128)S(1)}, f32[16,128,128]{2,1,0:T(8,128)S(1)}, f32[16,128,128]{2,1,0:T(8,128)S(1)}) fusion(f32[3]{0:T(128)S(1)} %copy-done.15, f32[3,16,128]{2,1,0:T(8,128)S(1)} %bitcast.72, f32[3,16,128]{2,1,0:T(8,128)S(1)} %bitcast.112, ...), kind=kLoop, calls=%fused_computation.10 | loop fusion | flops 14417920 | bytes 5341244 | tf_op jit(solution)/shard_map/reduce_sum | solution.py:43
  20.6 3.1 %fusion.132 = (f32[]{:T(128)}, f32[]{:T(128)}, f32[16,128,128]{2,1,0:T(8,128)S(1)}) fusion(f32[16,128,128]{2,1,0:T(8,128)S(1)} %get-tuple-element.475, f32[16,128]{1,0:T(8,128)S(1)} %bitcast.114, f32[16,128]{1,0:T(8,128)S(1)} %bitcast.138, f32[16,128]{1,0:T(8,128)S(1)} %bitcast.135, f32[16,128]{1,0:T(8,128)S(1)} %bitcast.132, f32[16,128]{1,0:T(8,128)S(1)} %bitcast.123, ...), kind=kLoop, calls=%fused_computation.314 | loop fusion | flops 13107198 | bytes 2162696 | tf_op jit(solution)/shard_map/reduce_sum | solution.py:74
  23.8 0.0 copy-start.7
  23.8 0.0 copy-start.8
  23.8 0.0 copy-start.9
  23.8 0.0 copy-start.10
  23.8 0.0 copy-start.11
  23.8 0.0 copy-start.12
  23.9 7.4 %fusion.160 = (f32[]{:T(128)}, f32[]{:T(128)}, f32[]{:T(128)}, f32[]{:T(128)}, f32[]{:T(128)}, /*index=5*/f32[]{:T(128)}, f32[16,128,128]{2,1,0:T(8,128)S(1)}, f32[16,128,128]{2,1,0:T(8,128)S(1)}, f32[16,128,128]{2,1,0:T(8,128)S(1)}) fusion(f32[16,128,128]{2,1,0:T(8,128)S(1)} %get-tuple-element.471, f32[16,128]{1,0:T(8,128)S(1)} %bitcast.124, ...), kind=kLoop, calls=%fused_computation.342 | loop fusion | flops 39321596 | bytes 6389784 | tf_op jit(solution)/shard_map/reduce_sum | solution.py:74
  31.3 8.2 %multiply_reduce_fusion = (f32[16,128,128]{2,1,0:T(8,128)S(1)}, f32[16,128,128]{2,1,0:T(8,128)S(1)}, f32[3,16,128]{2,1,0:T(8,128)}, f32[3,16,128]{2,1,0:T(8,128)...) fusion(f32[3]{0:T(128)S(1)} %copy-done.11, ...), kind=kLoop, calls=%fused_computation.5 | loop fusion | flops 29061120 | bytes 9756780 | tf_op jit(solution)/shard_map/reduce_sum | solution.py:43
  39.5 7.4 %fusion.146 = (f32[]{:T(128)}, f32[]{:T(128)}, f32[]{:T(128)}, f32[]{:T(128)}, f32[]{:T(128)}, /*index=5*/f32[]{:T(128)}, f32[16,128,128]{2,1,0:T(8,128)S(1)}, f32[16,128,128]{2,1,0:T(8,128)S(1)}, f32[16,128,128]{2,1,0:T(8,128)S(1)}) fusion(f32[16,128,128]{2,1,0:T(8,128)S(1)} %get-tuple-element.470, f32[16,128]{1,0:T(8,128)S(1)} %bitcast.115, ...), kind=kLoop, calls=%fused_computation.328 | loop fusion | flops 39321596 | bytes 6389784 | tf_op jit(solution)/shard_map/reduce_sum | solution.py:74
  47.0 0.0 copy-start.4
  47.0 4.8 %rsqrt_multiply_fusion.31 = (f32[16,128,128]{2,1,0:T(8,128)S(1)}, f32[16,128,128]{2,1,0:T(8,128)S(1)}, f32[16,128,128]{2,1,0:T(8,128)S(1)}) fusion(f32[16,128,128]{2,1,0:T(8,128)S(1)} %get-tuple-element.468, f32[16,128]{1,0:T(8,128)S(1)} %bitcast.147, f32[16,128]{1,0:T(8,128)S(1)} %bitcast.144, f32[16,128]{1,0:T(8,128)S(1)} %bitcast.141, ...), kind=kLoop, calls=%fused_computation.241 | loop fusion | flops 27525120 | bytes 6389760 | tf_op jit(solution)/shard_map/mul | solution.py:72
  51.8 10.2 %fusion.4 = (f32[3,16,128]{2,1,0:T(8,128)S(1)}, f32[3,16,128]{2,1,0:T(8,128)S(1)}, f32[16,128,128]{2,1,0:T(8,128)S(1)}, f32[3,16,128]{2,1,0:T(8,128)S(1)}, f32[3...) fusion(f32[16,128,128]{2,1,0:T(8,128)S(1)} %get-tuple-element.5, ...), kind=kLoop, calls=%fused_computation.8 | loop fusion | flops 31383552 | bytes 9879636 | tf_op jit(solution)/shard_map/reduce_sum | solution.py:74
  62.1 4.9 %fusion.167 = (f32[]{:T(128)}, f32[]{:T(128)}, f32[]{:T(128)}, f32[]{:T(128)}, f32[16,128,128]{2,1,0:T(8,128)S(1)}) fusion(f32[16,128,128]{2,1,0:T(8,128)S(1)} %get-tuple-element.459, f32[16,128]{1,0:T(8,128)S(1)} %bitcast.148, f32[16,128]{1,0:T(8,128)S(1)} %bitcast.145, f32[16,128]{1,0:T(8,128)S(1)} %bitcast.142, f32[16,128]{1,0:T(8,128)S(1)} %bitcast.130, ...), kind=kLoop, calls=%fused_computation.349 | loop fusion | flops 23855100 | bytes 4292624 | tf_op jit(solution)/shard_map/reduce_sum | solution.py:74
  67.0 7.0 %fusion.153 = (f32[]{:T(128)}, f32[]{:T(128)}, f32[]{:T(128)}, f32[]{:T(128)}, f32[]{:T(128)}, /*index=5*/f32[]{:T(128)}, f32[16,128,128]{2,1,0:T(8,128)S(1)}, f32[16,128,128]{2,1,0:T(8,128)S(1)}) fusion(f32[16,128,128]{2,1,0:T(8,128)S(1)} %get-tuple-element.460, f32[16,128]{1,0:T(8,128)S(1)} %bitcast.125, f32[16,128]{1,0:T(8,128)S(1)} %bitcast.122, ...), kind=kLoop, calls=%fused_computation.335 | loop fusion | flops 37224444 | bytes 6455320 | tf_op jit(solution)/shard_map/reduce_sum | solution.py:74
  74.0 4.6 %fusion.125 = (f32[]{:T(128)}, f32[]{:T(128)}, f32[]{:T(128)}, f32[]{:T(128)}, f32[16,128,128]{2,1,0:T(8,128)S(1)}) fusion(f32[16,128,128]{2,1,0:T(8,128)S(1)} %get-tuple-element.457, f32[16,128]{1,0:T(8,128)S(1)} %bitcast.192, f32[16,128]{1,0:T(8,128)S(1)} %bitcast.193, f32[16,128]{1,0:T(8,128)S(1)} %bitcast.194, f32[16,128]{1,0:T(8,128)S(1)} %bitcast.191, ...), kind=kLoop, calls=%fused_computation.307 | loop fusion | flops 23855100 | bytes 4292624 | tf_op jit(solution)/shard_map/reduce_sum | solution.py:74
  78.6 3.1 %fusion.22 = (f32[3,16,128]{2,1,0:T(8,128)S(1)}, f32[3,16,128]{2,1,0:T(8,128)S(1)}, f32[3,16,128]{2,1,0:T(8,128)S(1)}, f32[3,16,128]{2,1,0:T(8,128)S(1)}) fusion(f32[16,128,128]{2,1,0:T(8,128)S(1)} %get-tuple-element.489, f32[3,16,128]{2,1,0:T(8,128)S(1)} %bitcast.107, f32[3,16,128]{2,1,0:T(8,128)S(1)} %bitcast.82, f32[16,128,128]{2,1,0:T(8,128)S(1)} %get-tuple-element.497), kind=kLoop, calls=%fused_computation.38 | loop fusion | flops 7053312 | bytes 2244608 | tf_op jit(solution)/shard_map/reduce_sum | solution.py:74
  81.7 0.6 neg.108
  82.6 0.2 scatter-add.119
  82.9 0.8 fusion.319
  83.6 0.8 slice_add_fusion.16
  84.4 0.2 scatter-add.121
  84.7 0.2 scatter-add.125
  85.0 0.2 scatter-add.129
  85.2 0.0 copy-start.2
  85.2 5.0 %fusion.10 = (f32[3,16,128]{2,1,0:T(8,128)S(1)}, f32[3,16,128]{2,1,0:T(8,128)S(1)}, f32[3,16,128]{2,1,0:T(8,128)S(1)}, f32[3,16,128]{2,1,0:T(8,128)S(1)}, f32[3,...) fusion(f32[16,128,128]{2,1,0:T(8,128)S(1)} %get-tuple-element.496, f32[3]{0:T(128)S(1)} %copy-done.12, ...), kind=kLoop, calls=%fused_computation.18 | loop fusion | flops 11759616 | bytes 3366948 | tf_op jit(solution)/shard_map/reduce_sum | solution.py:74
  90.4 0.2 scatter-add.135
  90.7 0.2 scatter-add.139
  91.0 0.2 scatter-add.141
  91.2 0.0 copy-done.2
  91.3 0.2 scatter-add.145
  91.6 0.2 scatter-add.149
  91.8 0.4 collective-permute-start.3
  92.2 5.6 %collective-permute-done.3 = f32[3,3,5,1,128]{4,3,2,1,0:T(1,128)S(1)} collective-permute-done((f32[3,3,5,1,128]{4,3,2,1,0:T(1,128)S(1)}, f32[3,3,5,1,128]{4,3,2,1,0:T(1,128)S(1)}, u32[]{:S(2)}, u32[]{:S(2)}) %collective-permute-start.3) | collective-permute-done | bytes 23072 | tf_op jit(solution)/shard_map/ppermute | solution.py:18
  97.8 0.1 scatter-add.150
  98.0 0.1 collective-permute-start.4
  115.7 40.4 %all-reduce.1 = (f32[1]{0:T(128)}, f32[1]{0:T(128)}) all-reduce(f32[1]{0:T(128)} %bitcast.71, f32[1]{0:T(128)} %bitcast.70), channel_id=1, replica_groups=mesh['gx'=4,'gy'=2,'gz'=4] {'gx','gy','gz'}, use_global_device_ids=true, to_apply=%region_74.0 | all-reduce | flops 2 | bytes 16 | tf_op jit(solution)/shard_map/psum | solution.py:122
  156.1 0.0 collective-permute-done.4
  156.1 2.3 %collective-permute-start.5 = (f32[3,1,4,2,128]{4,3,2,1,0:T(2,128)S(1)}, f32[3,1,4,2,128]{4,3,2,1,0:T(2,128)S(1)}, u32[]{:S(2)}, u32[]{:S(2)}) collective-permute-start(f32[3,1,4,2,128]{4,3,2,1,0:T(2,128)S(1)} %slice.1711), channel_id=1, source_target_pairs={{0,8},{8,16},{16,24},{24,0},{1,9},{9,17},{17,25},{25,1},{2,10},{10... | collective-permute-start | bytes 36872 | tf_op jit(solution)/shard_map/ppermute | solution.py:18
  158.4 1.9 %maximum_multiply_fusion = f32[2]{0:T(128)} fusion(f32[1]{0:T(128)} %get-tuple-element.485, f32[1]{0:T(128)} %get-tuple-element.486), kind=kLoop, calls=%fused_computation.665 | loop fusion | flops 4 | bytes 16 | tf_op jit(solution)/shard_map/mul | solution.py:132
  160.4 0.4 collective-permute-done.5
  160.8 0.6 copy-done.3
  (84 shorter events, 1.3 us)
Async XLA Ops:
  0.6 16.4 %copy-start.5 = (f32[3]{0:T(128)S(1)}, f32[3]{0:T(128)}, u32[]{:S(2)}) copy-start(f32[3]{0:T(128)} %constant.879.clone) | copy-start | bytes 40
  0.6 16.4 %copy-start.13 = (f32[3]{0:T(128)S(1)}, f32[3]{0:T(128)}, u32[]{:S(2)}) copy-start(f32[3]{0:T(128)} %constant.880.clone) | copy-start | bytes 40
  0.7 16.4 %copy-start.14 = (f32[3]{0:T(128)S(1)}, f32[3]{0:T(128)}, u32[]{:S(2)}) copy-start(f32[3]{0:T(128)} %constant.883.clone) | copy-start | bytes 40
  0.7 16.4 %copy-start.6 = (f32[3]{0:T(128)S(1)}, f32[3]{0:T(128)}, u32[]{:S(2)}) copy-start(f32[3]{0:T(128)} %constant.886.clone) | copy-start | bytes 40
  0.7 16.4 %copy-start.15 = (f32[3]{0:T(128)S(1)}, f32[3]{0:T(128)}, u32[]{:S(2)}) copy-start(f32[3]{0:T(128)} %constant.890.clone) | copy-start | bytes 40
  0.7 16.4 %copy-start = (f32[3,2,4,2,128]{4,3,2,1,0:T(2,128)S(1)}, f32[3,2,4,2,128]{4,3,2,1,0:T(2,128)}, u32[]{:S(2)}) copy-start(f32[3,2,4,2,128]{4,3,2,1,0:T(2,128)} %param.82) | copy-start | bytes 73732
  4.5 5.5 %collective-permute-start = (f32[7,1,4,2,128]{4,3,2,1,0:T(2,128)S(1)}, f32[7,1,4,2,128]{4,3,2,1,0:T(2,128)S(1)}, u32[]{:S(2)}, u32[]{:S(2)}) collective-permute-start(f32[7,1,4,2,128]{4,3,2,1,0:T(2,128)S(1)} %slice.1661), channel_id=1, source_target_pairs={{0,24},{8,0},{16,8},{24,16},{1,25},{9,1},{17,9},{25,17},{2,26},{10... | collective-permute-start | bytes 86024 | tf_op jit(solution)/shard_map/ppermute | solution.py:18
  10.1 1.3 collective-permute-start.1
  11.4 5.5 %collective-permute-start.2 = (f32[7,3,5,1,128]{4,3,2,1,0:T(1,128)S(1)}, f32[7,3,5,1,128]{4,3,2,1,0:T(1,128)S(1)}, u32[]{:S(2)}, u32[]{:S(2)}) collective-permute-start(f32[7,3,5,1,128]{4,3,2,1,0:T(1,128)S(1)} %slice.1680), channel_id=1, source_target_pairs={{0,3},{1,0},{2,1},{3,2},{4,7},{5,4},{6,5},{7,6},{8,11},{9,8},{10,9... | collective-permute-start | bytes 161288 | tf_op jit(solution)/shard_map/ppermute | solution.py:18
  23.8 7.5 %copy-start.7 = (f32[3]{0:T(128)S(1)}, f32[3]{0:T(128)}, u32[]{:S(2)}) copy-start(f32[3]{0:T(128)} %constant.881.clone) | copy-start | bytes 40
  23.8 7.5 %copy-start.8 = (f32[3]{0:T(128)S(1)}, f32[3]{0:T(128)}, u32[]{:S(2)}) copy-start(f32[3]{0:T(128)} %constant.882.clone) | copy-start | bytes 40
  23.8 7.5 %copy-start.9 = (f32[3]{0:T(128)S(1)}, f32[3]{0:T(128)}, u32[]{:S(2)}) copy-start(f32[3]{0:T(128)} %constant.884.clone) | copy-start | bytes 40
  23.8 7.4 %copy-start.10 = (f32[3]{0:T(128)S(1)}, f32[3]{0:T(128)}, u32[]{:S(2)}) copy-start(f32[3]{0:T(128)} %constant.888.clone) | copy-start | bytes 40
  23.8 7.4 %copy-start.11 = (f32[3]{0:T(128)S(1)}, f32[3]{0:T(128)}, u32[]{:S(2)}) copy-start(f32[3]{0:T(128)} %constant.891.clone) | copy-start | bytes 40
  23.8 7.4 %copy-start.12 = (f32[3]{0:T(128)S(1)}, f32[3]{0:T(128)}, u32[]{:S(2)}) copy-start(f32[3]{0:T(128)} %constant.889.clone) | copy-start | bytes 40
  47.0 4.8 %copy-start.4 = (f32[3]{0:T(128)S(1)}, f32[3]{0:T(128)}, u32[]{:S(2)}) copy-start(f32[3]{0:T(128)} %constant.887.clone) | copy-start | bytes 40
  85.2 6.0 %copy-start.1 = (f32[3,16,128]{2,1,0:T(8,128)S(1)}, f32[3,16,128]{2,1,0:T(8,128)}, u32[]{:S(2)}) copy-start(f32[3,16,128]{2,1,0:T(8,128)} %get-tuple-element.462) | copy-start | bytes 73732
  85.2 6.0 %copy-start.2 = (f32[3,16,128]{2,1,0:T(8,128)S(1)}, f32[3,16,128]{2,1,0:T(8,128)}, u32[]{:S(2)}) copy-start(f32[3,16,128]{2,1,0:T(8,128)} %get-tuple-element.461) | copy-start | bytes 73732
  91.8 6.0 %collective-permute-start.3 = (f32[3,3,5,1,128]{4,3,2,1,0:T(1,128)S(1)}, f32[3,3,5,1,128]{4,3,2,1,0:T(1,128)S(1)}, u32[]{:S(2)}, u32[]{:S(2)}) collective-permute-start(f32[3,3,5,1,128]{4,3,2,1,0:T(1,128)S(1)} %slice.1705), channel_id=1, source_target_pairs={{0,1},{1,2},{2,3},{3,0},{4,5},{5,6},{6,7},{7,4},{8,9},{9,10},{10,1... | collective-permute-start | bytes 69128 | tf_op jit(solution)/shard_map/ppermute | solution.py:18
  98.0 58.1 %collective-permute-start.4 = (f32[3,3,1,2,128]{4,3,2,1,0:T(2,128)S(1)}, f32[3,3,1,2,128]{4,3,2,1,0:T(2,128)S(1)}, u32[]{:S(2)}, u32[]{:S(2)}) collective-permute-start(f32[3,3,1,2,128]{4,3,2,1,0:T(2,128)S(1)} %slice.1708), channel_id=1, source_target_pairs={{0,4},{4,0},{1,5},{5,1},{2,6},{6,2},{3,7},{7,3},{8,12},{12,8},{9,1... | collective-permute-start | bytes 27656 | tf_op jit(solution)/shard_map/ppermute | solution.py:18
  156.1 4.6 %collective-permute-start.5 = (f32[3,1,4,2,128]{4,3,2,1,0:T(2,128)S(1)}, f32[3,1,4,2,128]{4,3,2,1,0:T(2,128)S(1)}, u32[]{:S(2)}, u32[]{:S(2)}) collective-permute-start(f32[3,1,4,2,128]{4,3,2,1,0:T(2,128)S(1)} %slice.1711), channel_id=1, source_target_pairs={{0,8},{8,16},{16,24},{24,0},{1,9},{9,17},{17,25},{25,1},{2,10},{10... | collective-permute-start | bytes 36872 | tf_op jit(solution)/shard_map/ppermute | solution.py:18
  160.8 0.6 copy-start.3
where the time goes:
time: 162 us; the launch traced here: 161 us
  other arithmetic  75.3 us (46%)
  blocking collectives  40.4 us (25%)
  between operations  19 us (12%)
  starting transfers between devices  10.5 us (6%)
  waiting for transfers between devices  10.3 us (6%)
  local copies, waits for them, and re-layouts  5.94 us (4%)
    psum x1, blocking collectives, per_device(): summed = lax.psum((energy, virial), ('gx', 'gy', 'gz'))  40.4 us
    reduce_sum x6, other arithmetic, pair_terms(): jnp.sum(energy)  34.4 us
    reduce_sum x3, other arithmetic, pair_terms(): jnp.sum(weighted, 2)  18.3 us
    reduce_sum x2, other arithmetic, pair_terms(): dist_sq = jnp.sum(displace * displace, 0)  11.7 us
    ppermute x6, starting transfers between devices, passed_along(): return lax.ppermute(value, axis, pairs)  10.5 us
    ppermute x6, waiting for transfers between devices, passed_along(): return lax.ppermute(value, axis, pairs)  10.3 us
    mul x1, other arithmetic, pair_terms(): slope = live_mask * (slope_here - slope_cut) * inverse  4.8 us
  transfers between devices with their start and end apart: 6, of which 5 were waited for; matrix products, arithmetic and copies ran while one was open for 1% of the time, Pallas kernels for 0%

commit v1 on v0

v1 whole, which is shorter than its diff:
```python
import functools

import jax
import jax.numpy as jnp
from jax import lax
from jax.experimental import pallas as pl
from jax.experimental.pallas import tpu as pltpu
from jax.sharding import PartitionSpec as P

MESH = pl.DeviceIdType.MESH
AXES = ("gx", "gy", "gz")
soft_core = 0.09
cut_sq = 1.0 + soft_core
cut_len = cut_sq**0.5
second_of = {0: (0, 1, 2, 3, 4, 5, 6, 7), 1: (2, 6), 2: (4, 5), 4: (1, 3)}
VMEM_LIMIT = 60 * 1024 * 1024


def corner_of(which):
    return (which & 1, which >> 1 & 1, which >> 2 & 1)


def neighbour(which, step):
    target = {}
    for axis, bit in zip(AXES, corner_of(which)):
        if bit:
            count = lax.axis_size(axis)
            target[axis] = lax.rem(lax.axis_index(axis) + step + count, count)
    return target


def halo_kernel(own, ext, send_sem, recv_sem):
    sizes = own.shape[:3]
    barrier = pltpu.get_barrier_semaphore()
    for which in range(1, 8):
        pl.semaphore_signal(barrier, inc=1, device_id=neighbour(which, 1), device_id_type=MESH)
    ext[: sizes[0], : sizes[1], : sizes[2]] = own[...]
    pl.semaphore_wait(barrier, 7)
    copies = []
    for which in range(1, 8):
        bits = corner_of(which)
        source = tuple(pl.ds(0, 1 if bit else size) for bit, size in zip(bits, sizes))
        target = tuple(
            pl.ds(size, 1) if bit else pl.ds(0, size) for bit, size in zip(bits, sizes)
        )
        copy = pltpu.make_async_remote_copy(
            src_ref=own.at[source],
            dst_ref=ext.at[target],
            send_sem=send_sem.at[which],
            recv_sem=recv_sem.at[which],
            device_id=neighbour(which, -1),
            device_id_type=MESH,
        )
        copy.start()
        copies.append(copy)
    for copy in copies:
        copy.wait()


def pair_kernel(types, ext, reaction, totals, rows, first, table, force_i, force_j):
    ext_sizes = ext.shape[:3]
    sizes = tuple(size - 1 for size in ext_sizes)
    width = ext.shape[-1]
    groups = width // 8
    per_cell = 3 + 5 * types
    cells = [
        (x, y, z)
        for x in range(ext_sizes[0])
        for y in range(ext_sizes[1])
        for z in range(ext_sizes[2])
    ]

    def index_of(x, y, z):
        return (x * ext_sizes[1] + y) * ext_sizes[2] + z

    pack = width // 4
    force_i[...] = jnp.zeros(force_i.shape, jnp.float32)
    force_j[...] = jnp.zeros(force_j.shape, jnp.float32)
    row_at = lax.broadcasted_iota(jnp.int32, (4, width), 0)
    for cell, (x, y, z) in enumerate(cells):
        base = jnp.where(row_at == 0, x, jnp.where(row_at == 1, y, jnp.where(row_at == 2, z, 0)))
        values = ext[x, y, z, 0:4] + base.astype(jnp.float32)
        for axis in range(3):
            table[cell, axis] = jnp.broadcast_to(values[axis : axis + 1], (8, width))
        parked = (row_at == 0) & (values[3:4] < 0.0)
        rows[pl.ds(4 * cell, 4)] = jnp.where(parked, x + 4.0, values)
        for kind in range(types):
            line = [
                jnp.broadcast_to(ext[x, y, z, pl.ds(4 + 4 * kind + at, 1)], (8, width))
                for at in range(4)
            ]
            for at in range(4):
                table[cell, 3 + 5 * kind + at] = line[at]
            table[cell, 3 + 5 * kind + 4] = cut_len * line[3] - (
                line[0] * (cut_sq**-6 / 12.0) - line[1] * (cut_sq**-3 / 6.0) + line[2] / cut_len
            )
    for cell, (x, y, z) in enumerate(cells):
        if cell % pack == 0:
            turned = jnp.transpose(rows[pl.ds(4 * cell, width)])
        if (x == sizes[0]) + (y == sizes[1]) + (z == sizes[2]) > 1:
            continue
        for axis in range(4):
            lane = 4 * (cell % pack) + axis
            first[cell, axis] = jnp.broadcast_to(
                turned[:, lane : lane + 1], (width, width)
            ).reshape((groups, 8, width))

    def interact(own, other, kinds, depth, ordered=None):
        xi, yi, zi = own
        second = [table[other, at][None] for at in range(per_cell)]

        def chosen(at):
            value = second[3 + at]
            for kind in range(1, types):
                value = jnp.where(kinds[kind - 1], second[3 + 5 * kind + at], value)
            return value

        dx, dy, dz = second[0] - xi, second[1] - yi, second[2] - zi
        soft_sq = jnp.minimum(dx * dx + dy * dy + dz * dz + soft_core, cut_sq)
        inverse = lax.rsqrt(soft_sq)
        inverse_2 = inverse * inverse
        inverse_6 = inverse_2 * inverse_2 * inverse_2
        twelve = chosen(0) * inverse_6 * inverse_6
        six = chosen(1) * inverse_6
        coulomb = chosen(2) * inverse
        shift = chosen(3) * (soft_sq * inverse)
        slope = ((six - twelve) - (coulomb + shift)) * inverse_2
        forces = (slope * dx, slope * dy, slope * dz)
        if ordered is None:
            for axis in range(3):
                force_j[other, axis] -= jnp.sum(forces[axis], 0)
            return forces, (twelve, six, coulomb, shift)
        value = twelve * (1.0 / 12.0) - six * (1.0 / 6.0) + coulomb - shift + chosen(4)
        return forces, jnp.sum(jnp.where(ordered, value, 0.0), 0)

    def one_cell(member, energy):
        z0 = lax.rem(member, sizes[2])
        y0 = lax.rem(member // sizes[2], sizes[1])
        x0 = member // (sizes[2] * sizes[1])

        def cell_at(which):
            shift = corner_of(which)
            return index_of(x0 + shift[0], y0 + shift[1], z0 + shift[2])

        for first_corner, seconds in second_of.items():
            depth = 2 if first_corner == 0 else 4
            here = cell_at(first_corner)
            others = [cell_at(which) for which in seconds]
            kind_row = rows[pl.ds(4 * here + 3, 1)]
            held = jnp.sum((kind_row >= 0.0).astype(jnp.int32))
            trips = (held + (8 * depth - 1)) // (8 * depth)
            tile = here // pack
            lane_at = lax.broadcasted_iota(jnp.int32, (1, 8, width), 2) - 4 * lax.rem(here, pack)
            slot_at = (
                lax.broadcasted_iota(jnp.int32, (depth, 8, width), 0) * 8
                + lax.broadcasted_iota(jnp.int32, (depth, 8, width), 1)
                - lax.broadcasted_iota(jnp.int32, (depth, 8, width), 2)
            )

            def step(at, carry, first_corner=first_corner, seconds=seconds, depth=depth,
                     here=here, others=others, tile=tile, lane_at=lane_at, slot_at=slot_at):
                energy, numbers = carry[0], list(carry[1:])
                span = pl.ds(at * depth, depth)
                own = tuple(first[here, axis, span] for axis in range(3))
                kind_at = first[here, 3, span]
                kinds = [kind_at == float(kind) for kind in range(1, types)]
                numbers = [
                    number + jnp.sum(kind.astype(jnp.float32), 0)
                    for number, kind in zip(numbers, kinds)
                ]
                total = None
                sums = None
                for which, other in zip(seconds, others):
                    if which == first_corner:
                        forces, own_energy = interact(
                            own, other, kinds, depth, slot_at + at * (8 * depth) < 0
                        )
                        energy = energy + own_energy
                    else:
                        forces, terms = interact(own, other, kinds, depth)
                        terms = [jnp.sum(term, 0) for term in terms]
                        sums = terms if sums is None else [a + b for a, b in zip(sums, terms)]
                    total = forces if total is None else [a + b for a, b in zip(total, forces)]
                energy = energy + (
                    (sums[0] * (1.0 / 12.0) - sums[1] * (1.0 / 6.0)) + (sums[2] - sums[3])
                )
                summed = [jnp.sum(value, 2, keepdims=True) for value in total]
                placed = jnp.where(
                    lane_at == 0,
                    summed[0],
                    jnp.where(
                        lane_at == 1, summed[1], jnp.where(lane_at == 2, summed[2], 0.0)
                    ),
                )
                force_i[tile, span] += placed
                return (energy, *numbers)

            zero = jnp.zeros((8, width), jnp.float32)
            energy, *numbers = lax.fori_loop(
                0, trips, step, (energy,) + (zero,) * (types - 1)
            )
            rest = jnp.full((8, width), (trips * depth).astype(jnp.float32))
            for number in numbers:
                rest = rest - number
            for which, other in zip(seconds, others):
                if which != first_corner:
                    for kind, number in enumerate([rest, *numbers]):
                        energy = energy + number * table[other, 3 + 5 * kind + 4]
        return energy

    members = sizes[0] * sizes[1] * sizes[2]
    energy = lax.fori_loop(0, members, one_cell, jnp.zeros((8, width), jnp.float32))

    virial = jnp.zeros((3, width), jnp.float32)
    turned = None
    reaction[...] = jnp.zeros(reaction.shape, jnp.float32)
    for cell, (x, y, z) in enumerate(cells):
        if cell % pack == 0:
            turned = jnp.transpose(force_i[cell // pack].reshape((width, width)))
        lane = 4 * (cell % pack)
        second_sum = jnp.concatenate(
            [jnp.sum(force_j[cell, axis], 0, keepdims=True) for axis in range(3)], 0
        )
        held = rows[pl.ds(4 * cell + 3, 1)] >= 0.0
        force = jnp.where(held, turned[lane : lane + 3] + second_sum, 0.0)
        reaction[x, y, z, 0:3] = force
        virial = virial - force * rows[pl.ds(4 * cell, 3)]
    totals[...] = jnp.zeros(totals.shape, jnp.float32)
    totals[0:1] = jnp.sum(energy, 0, keepdims=True)
    totals[1:2] = jnp.sum(virial, 0, keepdims=True)


def return_kernel(
    normaliser, reaction, part, forces, totals, *scratch
):
    ext_sizes = reaction.shape[:3]
    sizes = tuple(size - 1 for size in ext_sizes)
    landed = scratch[:7]
    send_sem, recv_sem, line, plane, middle, line_send, line_recv, plane_send, plane_recv = scratch[7:]
    count_x, count_y, count_z = (lax.axis_size(axis) for axis in AXES)
    at_x, at_y, at_z = (lax.axis_index(axis) for axis in AXES)
    count_plane = count_y * count_z
    at_plane = at_y * count_z + at_z

    def line_target(step):
        return {"gx": lax.rem(at_x + step, count_x)}

    def plane_target(step):
        spot = lax.rem(at_plane + step, count_plane)
        return {"gy": spot // count_z, "gz": lax.rem(spot, count_z)}

    barrier = pltpu.get_barrier_semaphore()
    for which in range(1, 8):
        pl.semaphore_signal(barrier, inc=1, device_id=neighbour(which, -1), device_id_type=MESH)
    for step in range(1, count_x):
        pl.semaphore_signal(barrier, inc=1, device_id=line_target(step), device_id_type=MESH)
    for step in range(1, count_plane):
        pl.semaphore_signal(barrier, inc=1, device_id=plane_target(step), device_id_type=MESH)
    pl.semaphore_wait(barrier, 7 + count_x - 1 + count_plane - 1)

    copies = []
    for which in range(1, 8):
        source = tuple(
            pl.ds(size, 1) if bit else pl.ds(0, size)
            for bit, size in zip(corner_of(which), sizes)
        )
        copy = pltpu.make_async_remote_copy(
            src_ref=reaction.at[source],
            dst_ref=landed[which - 1],
            send_sem=send_sem.at[which],
            recv_sem=recv_sem.at[which],
            device_id=neighbour(which, 1),
            device_id_type=MESH,
        )
        copy.start()
        copies.append(copy)
    line_copies = []
    for step in range(1, count_x):
        copy = pltpu.make_async_remote_copy(
            src_ref=part,
            dst_ref=line.at[at_x],
            send_sem=line_send.at[step],
            recv_sem=line_recv.at[step],
            device_id=line_target(step),
            device_id_type=MESH,
        )
        copy.start()
        line_copies.append(copy)
    line[at_x] = part[...]
    for copy in line_copies:
        copy.wait()
    summed = line[0]
    for step in range(1, count_x):
        summed = summed + line[step]
    middle[...] = summed
    plane[at_plane] = summed
    for copy in copies:
        copy.wait()
    for x in range(sizes[0]):
        for y in range(sizes[1]):
            for z in range(sizes[2]):
                value = reaction[x, y, z]
                for which in range(1, 8):
                    bits = corner_of(which)
                    spot = (x, y, z)
                    if all(not bit or at == 0 for bit, at in zip(bits, spot)):
                        value = value + landed[which - 1][
                            tuple(0 if bit else at for bit, at in zip(bits, spot))
                        ]
                for axis in range(3):
                    forces[axis, x, y, pl.ds(z, 1)] = value[axis : axis + 1]
    plane_copies = []
    for step in range(1, count_plane):
        copy = pltpu.make_async_remote_copy(
            src_ref=middle,
            dst_ref=plane.at[at_plane],
            send_sem=plane_send.at[step],
            recv_sem=plane_recv.at[step],
            device_id=plane_target(step),
            device_id_type=MESH,
        )
        copy.start()
        plane_copies.append(copy)
    for copy in plane_copies:
        copy.wait()
    summed = plane[0]
    for step in range(1, count_plane):
        summed = summed + plane[step]
    totals[0] = jnp.sum(summed[0:1]) * normaliser
    totals[1] = jnp.sum(summed[1:2]) * normaliser


def packed_rows(positions, type_ids, counts, type_charge, type_sigma, type_epsilon):
    types = type_charge.shape[0]
    shape = type_ids.shape
    occupied = lax.broadcasted_iota(jnp.int32, shape, 3) < counts[..., None]
    root = jnp.sqrt(type_epsilon)

    def of_type(values):
        picked = jnp.broadcast_to(values[0], shape)
        for kind in range(1, types):
            picked = jnp.where(type_ids == kind, values[kind], picked)
        return picked

    lines = [positions[0], positions[1], positions[2]]
    lines.append(jnp.where(occupied, type_ids.astype(jnp.float32), -1.0))
    for kind in range(types):
        sigma_pair = 0.5 * (type_sigma + type_sigma[kind])
        depth_pair = 4.0 * root * root[kind]
        coulomb = type_charge * type_charge[kind]
        sig_six = (sigma_pair * sigma_pair) ** 3
        six = 6.0 * depth_pair * sig_six
        twelve = 12.0 * depth_pair * sig_six * sig_six
        shift = ((six * cut_sq**-3 - twelve * cut_sq**-6) - coulomb / cut_len) / cut_len
        for values in (twelve, six, coulomb, shift):
            lines.append(jnp.where(occupied, of_type(values), 0.0))
    count = -(-len(lines) // 8) * 8
    lines += [jnp.zeros(shape, jnp.float32)] * (count - len(lines))
    return jnp.stack(lines, 3)


def per_device(positions, type_ids, counts, type_charge, type_sigma, type_epsilon):
    types = type_charge.shape[0]
    own = packed_rows(positions, type_ids, counts, type_charge, type_sigma, type_epsilon)
    sizes, (height, width) = own.shape[:3], own.shape[3:]
    ext_sizes = tuple(size + 1 for size in sizes)
    cells = ext_sizes[0] * ext_sizes[1] * ext_sizes[2]
    vmem = pl.BlockSpec(memory_space=pltpu.VMEM)
    smem = pl.BlockSpec(memory_space=pltpu.SMEM)
    f32 = jnp.float32
    ext = pl.pallas_call(
        halo_kernel,
        name="halo",
        out_shape=jax.ShapeDtypeStruct(ext_sizes + (height, width), f32),
        in_specs=[vmem],
        out_specs=vmem,
        scratch_shapes=[pltpu.SemaphoreType.DMA((8,)), pltpu.SemaphoreType.DMA((8,))],
        compiler_params=pltpu.CompilerParams(collective_id=0, has_side_effects=True),
    )(own)
    pack = width // 4
    tiles = -(-cells // pack)
    reaction, part = pl.pallas_call(
        functools.partial(pair_kernel, types),
        name="pairs",
        out_shape=(
            jax.ShapeDtypeStruct(ext_sizes + (8, width), f32),
            jax.ShapeDtypeStruct((8, width), f32),
        ),
        in_specs=[vmem],
        out_specs=(vmem, vmem),
        scratch_shapes=[
            pltpu.VMEM((tiles * width, width), f32),
            pltpu.VMEM((cells, 4, width // 8, 8, width), f32),
            pltpu.VMEM((cells, 3 + 5 * types, 8, width), f32),
            pltpu.VMEM((tiles, width // 8, 8, width), f32),
            pltpu.VMEM((cells, 3, 8, width), f32),
        ],
        compiler_params=pltpu.CompilerParams(vmem_limit_bytes=VMEM_LIMIT),
    )(ext)
    count_x, count_y, count_z = (lax.axis_size(axis) for axis in AXES)
    count_plane = count_y * count_z
    normaliser = 1.0 / (
        sizes[0] * count_x * sizes[1] * count_y * sizes[2] * count_z * width
    )
    landing = [
        pltpu.VMEM(
            tuple(1 if bit else size for bit, size in zip(corner_of(which), sizes)) + (8, width),
            f32,
        )
        for which in range(1, 8)
    ]
    forces, totals = pl.pallas_call(
        functools.partial(return_kernel, normaliser),
        name="giveback",
        out_shape=(
            jax.ShapeDtypeStruct((3,) + sizes + (width,), f32),
            jax.ShapeDtypeStruct((2,), f32),
        ),
        in_specs=[vmem, vmem],
        out_specs=(vmem, smem),
        scratch_shapes=landing
        + [
            pltpu.SemaphoreType.DMA((8,)),
            pltpu.SemaphoreType.DMA((8,)),
            pltpu.VMEM((count_x, 8, width), f32),
            pltpu.VMEM((count_plane, 8, width), f32),
            pltpu.VMEM((8, width), f32),
            pltpu.SemaphoreType.DMA((count_x,)),
            pltpu.SemaphoreType.DMA((count_x,)),
            pltpu.SemaphoreType.DMA((count_plane,)),
            pltpu.SemaphoreType.DMA((count_plane,)),
        ],
        compiler_params=pltpu.CompilerParams(collective_id=1, has_side_effects=True),
    )(reaction, part)
    return forces, totals


def solution(mesh):
    in_specs = (
        P(None, "gx", "gy", "gz", None),
        P("gx", "gy", "gz", None),
        P("gx", "gy", "gz"),
        P(),
        P(),
        P(),
    )
    out_specs = (P(None, "gx", "gy", "gz", None), P())
    return jax.shard_map(
        per_device, mesh=mesh, in_specs=in_specs, out_specs=out_specs, check_vma=False
    )
```

time: 162 us -> 107 us (0.66)
  Pallas kernels: 0 us -> 80.5 us
  other arithmetic: 75.3 us -> 12.9 us
  blocking collectives: 40.4 us -> 0 us
  between operations: 19 us -> 2 us
  starting transfers between devices: 10.5 us -> 0 us
  waiting for transfers between devices: 10.3 us -> 0 us
  local copies, waits for them, and re-layouts: 5.94 us -> 11 us
    pallas_call x0 -> x3, Pallas kernels: none -> 80.5 us  [the longest x1 51.9 us: per_device(): pl.pallas_call(functools.partial(pair_kernel, types), name='pairs', out_s...]
    reduce_sum x12 -> x0, other arithmetic: 65.1 us -> none  [the longest x6 34.4 us: pair_terms(): jnp.sum(energy)]
    psum x1 -> x0, blocking collectives: 40.4 us -> none  [per_device(): summed = lax.psum((energy, virial), ('gx', 'gy', 'gz'))]
    ppermute x6 -> x0, starting transfers between devices: 10.5 us -> none  [passed_along(): return lax.ppermute(value, axis, pairs)]
    select_n x0 -> x2, other arithmetic: none -> 10.3 us  [packed_rows(): lines.append(jnp.where(occupied, of_type(values), 0.0))]
    ppermute x6 -> x0, waiting for transfers between devices: 10.3 us -> none  [passed_along(): return lax.ppermute(value, axis, pairs)]
    mul x2 -> x0, other arithmetic: 6.72 us -> none  [the longest x1 4.8 us: pair_terms(): slope = live_mask * (slope_here - slope_cut) * inverse]
    slice x10 -> x8, local copies, waits for them, and re-layouts: 0.14 us -> 4.33 us  [the longest x4 2.56 us: of_type(): picked = jnp.where(type_ids == kind, values[kind], picked)]
  transfers between devices with their start and end apart: 6 -> 0, of which waited for: 5 -> 0; matrix products, arithmetic and copies ran while one was open for 1% -> 0% of each run, Pallas kernels for 0% -> 0%
where the time goes in v1:
time: 107 us; the launch traced here: 106 us
  Pallas kernels  80.5 us (75%)
  other arithmetic  12.9 us (12%)
  local copies, waits for them, and re-layouts  11 us (10%)
  between operations  2 us (2%)
    pallas_call x1, Pallas kernels, per_device(): pl.pallas_call(functools.partial(pair_kernel, types), name='pairs', out_s...  51.9 us
    pallas_call x1, Pallas kernels, per_device(): pl.pallas_call(functools.partial(return_kernel, normaliser), name='giveba...  16.7 us
    pallas_call x1, Pallas kernels, per_device(): pl.pallas_call(halo_kernel, name='halo', out_shape=jax.ShapeDtypeStruct(e...  11.9 us
    select_n x2, other arithmetic, packed_rows(): lines.append(jnp.where(occupied, of_type(values), 0.0))  10.3 us
    unnamed x17, local copies, waits for them, and re-layouts  4.61 us
    slice x4, local copies, waits for them, and re-layouts, of_type(): picked = jnp.where(type_ids == kind, values[kind], picked)  2.56 us
    div x1, other arithmetic, packed_rows(): (six * cut_sq ** (-3) - twelve * cut_sq ** (-6) - coulomb / cut_len) / cu...  2.56 us

profile of v1, /device:TPU:0, one launch (start us, length us, event | category | flops | bytes accessed | tf_op | source)
XLA Modules:
  0.0 106.4 jit_solution(3756517759873089231)
XLA Ops:
  0.6 0.7 sqrt.3
  1.3 0.6 fusion.8
  3.2 0.0 copy-start.2
  3.2 0.6 copy-done.2
  3.8 0.6 fusion.10
  4.4 0.0 copy-start.3
  4.4 0.7 copy-done.3
  5.1 0.6 fusion.9
  5.7 0.0 copy-start.5
  5.7 0.7 copy-done.5
  6.3 2.6 %subtract_multiply_fusion.1 = (f32[2]{0:T(128)S(1)}, f32[2]{0:T(128)S(1)}, f32[2]{0:T(128)S(1)}, f32[2]{0:T(128)S(1)}, f32[2]{0:T(128)S(1)}, /*index=5*/f32[2]{0:T(128)S(1)}, f32[2]{0:T(128)S(1)}, f32[2]{0:T(128)S(1)}) fusion(f32[2]{0:T(128)S(1)} %copy-done.2, f32[]{:T(128)} %bitcast.15, f32[2]{0:T(128)S(1)} %copy-done.3, f32[]{:T(128)} %bitcast.6, ...), kind=kLoop, calls=%fused_computation.17 | loop fusion | flops 72 | bytes 112 | tf_op jit(solution)/shard_map/div | solution.py:354
  8.9 0.7 fusion.3
  9.5 0.6 fusion.5
  10.2 0.6 fusion.7
  10.8 0.6 fusion.1
  11.4 0.0 copy-start.4
  11.5 0.0 copy-start.1
  11.5 0.7 copy-done.4
  12.1 0.0 copy-start
  12.1 0.1 copy.8
  12.2 0.0 copy-done.1
  12.2 1.3 %select_select_fusion = (f32[2,4,2,128]{3,2,1,0:T(2,128)S(1)}, pred[2,4,2,128]{3,2,1,0:T(4,128)(4,1)S(1)}, f32[2,4,2,128]{3,2,1,0:T(2,128)S(1)}) fusion(f32[]{:T(128)} %bitcast.40, f32[]{:T(128)} %bitcast.39, s32[2,4,2]{2,1,0:T(4,128)S(1)} %copy.8, s32[2,4,2,128]{3,2,1,0:T(2,128)S(1)} %copy-done.1), kind=kLoop, calls=%fused_computation | loop fusion | flops 12288 | bytes 26696 | tf_op jit(solution)/shard_map/jit(_where)/select_n | solution.py:356
  13.6 0.0 copy-done
  13.6 9.0 %select_select_fusion.1 = (f32[2,4,2,128]{3,2,1,0:T(2,128)S(1)}, f32[2,4,2,128]{3,2,1,0:T(2,128)S(1)}, f32[2,4,2,128]{3,2,1,0:T(2,128)S(1)}, f32[2,4,2,128]{3,2,...) fusion(pred[2,4,2,128]{3,2,1,0:T(4,128)(4,1)S(1)} %get-tuple-element.7,, ...), kind=kLoop, calls=%fused_computation.1 | loop fusion | flops 30720 | bytes 59512 | tf_op jit(solution)/shard_map/jit(_where)/select_n | solution.py:356
  22.6 1.4 %stack.43.own = f32[2,4,2,16,128]{4,3,2,1,0:T(8,128)} concatenate(f32[2,4,2,1,128]{4,3,2,1,0:T(1,128)S(1)} %bitcast.60, f32[2,4,2,1,128]{4,3,2,1,0:T(1,128)S(1)} %bitcast.61, f32[2,4,2,1,128]{4,3,2,1,0:T(1,128)S(1)} %bitcast.59, f32[2,4,2,1,128]{4,3,2,1,0:T(1,128)S(1)} %bitcast.58, f32[2,4,2,1,128]{4,3,2,1,0:T(1,128)S(1)} %bitcast.56, f32[2,4,2,1,128]{4,3,2,1,0:T(1,128)S(1)} %bitcast.55, ...), dimensions={3} | concatenate | bytes 262144 | tf_op jit(solution)/shard_map/stack | solution.py:359
  24.0 11.9 %halo.1.ext = f32[3,5,3,16,128]{4,3,2,1,0:T(8,128)} custom-call(f32[2,4,2,16,128]{4,3,2,1,0:T(8,128)} %stack.43.own), custom_call_target="tpu_custom_call" | custom-call | tf_op jit(solution)/shard_map/halo/pallas_call | solution.py:371
  35.9 51.9 %pairs.1 = (f32[3,5,3,8,128]{4,3,2,1,0:T(8,128)}, f32[8,128]{1,0:T(8,128)}) custom-call(f32[3,5,3,16,128]{4,3,2,1,0:T(8,128)} %halo.1.ext), custom_call_target="tpu_custom_call" | custom-call | tf_op jit(solution)/shard_map/pairs/pallas_call | solution.py:382
  87.8 16.7 %giveback.1 = (f32[3,2,4,2,128]{4,3,2,1,0:T(2,128)}, f32[2]{0:T(128)}) custom-call(f32[3,5,3,8,128]{4,3,2,1,0:T(8,128)} %get-tuple-element.4.reaction, f32[8,128]{1,0:T(8,128)} %get-tuple-element.5.part), custom_call_target="tpu_custom_call" | custom-call | tf_op jit(solution)/shard_map/giveback/pallas_call | solution.py:412
  104.6 0.0 copy-start.6
  104.6 1.3 %copy.19 = f32[3,2,4,2,128]{4,3,2,1,0:T(2,128)} copy(f32[3,2,4,2,128]{4,3,2,1,0:T(2,128)} %get-tuple-element.63) | data formatting | bytes 49152
  105.9 0.0 copy-done.6
  105.9 0.5 copy.20
  (2 shorter events, 0.0 us)
Async XLA Ops:
  3.2 0.7 copy-start.2
  4.4 0.7 copy-start.3
  5.7 0.7 copy-start.5
  11.4 0.7 copy-start.4
  11.5 0.8 copy-start.1
  12.1 1.4 %copy-start = (f32[3,2,4,2,128]{4,3,2,1,0:T(2,128)S(1)}, f32[3,2,4,2,128]{4,3,2,1,0:T(2,128)}, u32[]{:S(2)}) copy-start(f32[3,2,4,2,128]{4,3,2,1,0:T(2,128)} %param.6) | copy-start | bytes 73732
  104.6 1.4 %copy-start.6 = (f32[2]{0:T(128)S(1)}, f32[2]{0:T(128)}, u32[]{:S(2)}) copy-start(f32[2]{0:T(128)} %get-tuple-element.64) | copy-start | bytes 28

commit v2 on v1

--- a/solution.py
+++ b/solution.py
@@ -13,7 +13,7 @@
 cut_sq = 1.0 + soft_core
 cut_len = cut_sq**0.5
 second_of = {0: (0, 1, 2, 3, 4, 5, 6, 7), 1: (2, 6), 2: (4, 5), 4: (1, 3)}
-VMEM_LIMIT = 60 * 1024 * 1024
+VMEM_LIMIT = 40 * 1024 * 1024
 
 
 def corner_of(which):
@@ -29,12 +29,23 @@
     return target
 
 
-def halo_kernel(own, ext, send_sem, recv_sem):
+def halo_kernel(positions, type_ids, counts, ext, own, send_sem, recv_sem):
     sizes = own.shape[:3]
+    width = own.shape[-1]
     barrier = pltpu.get_barrier_semaphore()
     for which in range(1, 8):
         pl.semaphore_signal(barrier, inc=1, device_id=neighbour(which, 1), device_id_type=MESH)
-    ext[: sizes[0], : sizes[1], : sizes[2]] = own[...]
+    slot = lax.broadcasted_iota(jnp.int32, (1, width), 1)
+    blank = jnp.zeros((4, width), jnp.float32)
+    for x in range(sizes[0]):
+        for y in range(sizes[1]):
+            for z in range(sizes[2]):
+                kind = type_ids[x, y, pl.ds(z, 1)].astype(jnp.float32)
+                lines = [positions[axis, x, y, pl.ds(z, 1)] for axis in range(3)]
+                lines.append(jnp.where(slot < counts[x, y, z], kind, -1.0))
+                tile = jnp.concatenate(lines + [blank], 0)
+                own[x, y, z] = tile
+                ext[x, y, z] = tile
     pl.semaphore_wait(barrier, 7)
     copies = []
     for which in range(1, 8):
@@ -57,7 +68,34 @@
         copy.wait()
 
 
-def pair_kernel(types, ext, reaction, totals, rows, first, table, force_i, force_j):
+def type_tables(types, shape, charges, sigmas, epsilons):
+    def full(value):
+        return jnp.full(shape, value, jnp.float32)
+
+    charge = [full(charges[kind]) for kind in range(types)]
+    sigma = [full(sigmas[kind]) for kind in range(types)]
+    root = [jnp.sqrt(full(epsilons[kind])) for kind in range(types)]
+    tables = {}
+    for a in range(types):
+        for b in range(types):
+            sigma_pair = 0.5 * (sigma[a] + sigma[b])
+            depth_pair = 4.0 * root[a] * root[b]
+            coulomb = charge[a] * charge[b]
+            square = sigma_pair * sigma_pair
+            sig_six = square * square * square
+            six = 6.0 * depth_pair * sig_six
+            twelve = 12.0 * depth_pair * sig_six * sig_six
+            cut_six, cut_twelve, cut_coulomb = six * cut_sq**-3, twelve * cut_sq**-6, coulomb / cut_len
+            shift = ((cut_six - cut_twelve) - cut_coulomb) / cut_len
+            level = cut_len * shift - (cut_twelve / 12.0 - cut_six / 6.0 + cut_coulomb)
+            tables[a, b] = (twelve, six, coulomb, shift, level)
+    return tables
+
+
+def pair_kernel(
+    types, charges, sigmas, epsilons, ext, reaction, totals,
+    rows, first, table, force_i, force_j, held_of,
+):
     ext_sizes = ext.shape[:3]
     sizes = tuple(size - 1 for size in ext_sizes)
     width = ext.shape[-1]
@@ -74,26 +112,25 @@
         return (x * ext_sizes[1] + y) * ext_sizes[2] + z
 
     pack = width // 4
-    force_i[...] = jnp.zeros(force_i.shape, jnp.float32)
     force_j[...] = jnp.zeros(force_j.shape, jnp.float32)
     row_at = lax.broadcasted_iota(jnp.int32, (4, width), 0)
+    tables = type_tables(types, (8, width), charges, sigmas, epsilons)
     for cell, (x, y, z) in enumerate(cells):
         base = jnp.where(row_at == 0, x, jnp.where(row_at == 1, y, jnp.where(row_at == 2, z, 0)))
         values = ext[x, y, z, 0:4] + base.astype(jnp.float32)
+        held_of[cell] = jnp.sum((values[3:4] >= 0.0).astype(jnp.int32))
         for axis in range(3):
             table[cell, axis] = jnp.broadcast_to(values[axis : axis + 1], (8, width))
         parked = (row_at == 0) & (values[3:4] < 0.0)
         rows[pl.ds(4 * cell, 4)] = jnp.where(parked, x + 4.0, values)
+        kind_row = jnp.broadcast_to(values[3:4], (8, width))
+        same = [kind_row == float(kind) for kind in range(types)]
         for kind in range(types):
-            line = [
-                jnp.broadcast_to(ext[x, y, z, pl.ds(4 + 4 * kind + at, 1)], (8, width))
-                for at in range(4)
-            ]
-            for at in range(4):
-                table[cell, 3 + 5 * kind + at] = line[at]
-            table[cell, 3 + 5 * kind + 4] = cut_len * line[3] - (
-                line[0] * (cut_sq**-6 / 12.0) - line[1] * (cut_sq**-3 / 6.0) + line[2] / cut_len
-            )
+            for at in range(5):
+                picked = jnp.zeros((8, width), jnp.float32)
+                for second_kind in range(types):
+                    picked = jnp.where(same[second_kind], tables[kind, second_kind][at], picked)
+                table[cell, 3 + 5 * kind + at] = picked
     for cell, (x, y, z) in enumerate(cells):
         if cell % pack == 0:
             turned = jnp.transpose(rows[pl.ds(4 * cell, width)])
@@ -146,11 +183,8 @@
             depth = 2 if first_corner == 0 else 4
             here = cell_at(first_corner)
             others = [cell_at(which) for which in seconds]
-            kind_row = rows[pl.ds(4 * here + 3, 1)]
-            held = jnp.sum((kind_row >= 0.0).astype(jnp.int32))
-            trips = (held + (8 * depth - 1)) // (8 * depth)
-            tile = here // pack
-            lane_at = lax.broadcasted_iota(jnp.int32, (1, 8, width), 2) - 4 * lax.rem(here, pack)
+            trips = (held_of[here] + (8 * depth - 1)) // (8 * depth)
+            part_at = tuple(second_of).index(first_corner)
             slot_at = (
                 lax.broadcasted_iota(jnp.int32, (depth, 8, width), 0) * 8
                 + lax.broadcasted_iota(jnp.int32, (depth, 8, width), 1)
@@ -158,7 +192,7 @@
             )
 
             def step(at, carry, first_corner=first_corner, seconds=seconds, depth=depth,
-                     here=here, others=others, tile=tile, lane_at=lane_at, slot_at=slot_at):
+                     here=here, others=others, part_at=part_at, slot_at=slot_at):
                 energy, numbers = carry[0], list(carry[1:])
                 span = pl.ds(at * depth, depth)
                 own = tuple(first[here, axis, span] for axis in range(3))
@@ -184,15 +218,8 @@
                 energy = energy + (
                     (sums[0] * (1.0 / 12.0) - sums[1] * (1.0 / 6.0)) + (sums[2] - sums[3])
                 )
-                summed = [jnp.sum(value, 2, keepdims=True) for value in total]
-                placed = jnp.where(
-                    lane_at == 0,
-                    summed[0],
-                    jnp.where(
-                        lane_at == 1, summed[1], jnp.where(lane_at == 2, summed[2], 0.0)
-                    ),
-                )
-                force_i[tile, span] += placed
+                for axis in range(3):
+                    force_i[part_at, member, axis, span] = total[axis]
                 return (energy, *numbers)
 
             zero = jnp.zeros((8, width), jnp.float32)
@@ -212,17 +239,32 @@
     energy = lax.fori_loop(0, members, one_cell, jnp.zeros((8, width), jnp.float32))
 
     virial = jnp.zeros((3, width), jnp.float32)
-    turned = None
+    ones = jnp.ones((8, 2 * width), jnp.bfloat16)
     reaction[...] = jnp.zeros(reaction.shape, jnp.float32)
     for cell, (x, y, z) in enumerate(cells):
-        if cell % pack == 0:
-            turned = jnp.transpose(force_i[cell // pack].reshape((width, width)))
-        lane = 4 * (cell % pack)
-        second_sum = jnp.concatenate(
-            [jnp.sum(force_j[cell, axis], 0, keepdims=True) for axis in range(3)], 0
-        )
         held = rows[pl.ds(4 * cell + 3, 1)] >= 0.0
-        force = jnp.where(held, turned[lane : lane + 3] + second_sum, 0.0)
+        lines = []
+        for axis in range(3):
+            line = jnp.sum(force_j[cell, axis], 0, keepdims=True)
+            partial = None
+            for part_at, first_corner in enumerate(second_of):
+                spot = [at - bit for at, bit in zip((x, y, z), corner_of(first_corner))]
+                if all(0 <= at < size for at, size in zip(spot, sizes)):
+                    member = (spot[0] * sizes[1] + spot[1]) * sizes[2] + spot[2]
+                    value = force_i[part_at, member, axis].reshape((width, width))
+                    partial = value if partial is None else partial + value
+            if partial is not None:
+                high = partial.astype(jnp.bfloat16)
+                low = (partial - high.astype(jnp.float32)).astype(jnp.bfloat16)
+                summed = lax.dot_general(
+                    ones,
+                    jnp.concatenate([high, low], 1),
+                    (((1,), (1,)), ((), ())),
+                    preferred_element_type=jnp.float32,
+                )
+                line = line + summed[0:1]
+            lines.append(jnp.where(held, line, 0.0))
+        force = jnp.concatenate(lines, 0)
         reaction[x, y, z, 0:3] = force
         virial = virial - force * rows[pl.ds(4 * cell, 3)]
     totals[...] = jnp.zeros(totals.shape, jnp.float32)
@@ -330,39 +372,9 @@
     totals[1] = jnp.sum(summed[1:2]) * normaliser
 
 
-def packed_rows(positions, type_ids, counts, type_charge, type_sigma, type_epsilon):
-    types = type_charge.shape[0]
-    shape = type_ids.shape
-    occupied = lax.broadcasted_iota(jnp.int32, shape, 3) < counts[..., None]
-    root = jnp.sqrt(type_epsilon)
-
-    def of_type(values):
-        picked = jnp.broadcast_to(values[0], shape)
-        for kind in range(1, types):
-            picked = jnp.where(type_ids == kind, values[kind], picked)
-        return picked
-
-    lines = [positions[0], positions[1], positions[2]]
-    lines.append(jnp.where(occupied, type_ids.astype(jnp.float32), -1.0))
-    for kind in range(types):
-        sigma_pair = 0.5 * (type_sigma + type_sigma[kind])
-        depth_pair = 4.0 * root * root[kind]
-        coulomb = type_charge * type_charge[kind]
-        sig_six = (sigma_pair * sigma_pair) ** 3
-        six = 6.0 * depth_pair * sig_six
-        twelve = 12.0 * depth_pair * sig_six * sig_six
-        shift = ((six * cut_sq**-3 - twelve * cut_sq**-6) - coulomb / cut_len) / cut_len
-        for values in (twelve, six, coulomb, shift):
-            lines.append(jnp.where(occupied, of_type(values), 0.0))
-    count = -(-len(lines) // 8) * 8
-    lines += [jnp.zeros(shape, jnp.float32)] * (count - len(lines))
-    return jnp.stack(lines, 3)
-
-
 def per_device(positions, type_ids, counts, type_charge, type_sigma, type_epsilon):
     types = type_charge.shape[0]
-    own = packed_rows(positions, type_ids, counts, type_charge, type_sigma, type_epsilon)
-    sizes, (height, width) = own.shape[:3], own.shape[3:]
+    sizes, width = type_ids.shape[:3], type_ids.shape[3]
     ext_sizes = tuple(size + 1 for size in sizes)
     cells = ext_sizes[0] * ext_sizes[1] * ext_sizes[2]
     vmem = pl.BlockSpec(memory_space=pltpu.VMEM)
@@ -371,12 +383,14 @@
     ext = pl.pallas_call(
         halo_kernel,
         name="halo",
-        out_shape=jax.ShapeDtypeStruct(ext_sizes + (height, width), f32),
-        in_specs=[vmem],
+        out_shape=jax.ShapeDtypeStruct(ext_sizes + (8, width), f32),
+        in_specs=[vmem, vmem, smem],
         out_specs=vmem,
-        scratch_shapes=[pltpu.SemaphoreType.DMA((8,)), pltpu.SemaphoreType.DMA((8,))],
-        compiler_params=pltpu.CompilerParams(collective_id=0, has_side_effects=True),
-    )(own)
+        scratch_shapes=[pltpu.VMEM(sizes + (8, width), f32), pltpu.SemaphoreType.DMA((8,)), pltpu.SemaphoreType.DMA((8,))],
+        compiler_params=pltpu.CompilerParams(
+            collective_id=0, has_side_effects=True, vmem_limit_bytes=8 * 1024 * 1024
+        ),
+    )(positions, type_ids, counts)
     pack = width // 4
     tiles = -(-cells // pack)
     reaction, part = pl.pallas_call(
@@ -386,17 +400,20 @@
             jax.ShapeDtypeStruct(ext_sizes + (8, width), f32),
             jax.ShapeDtypeStruct((8, width), f32),
         ),
-        in_specs=[vmem],
+        in_specs=[smem, smem, smem, vmem],
         out_specs=(vmem, vmem),
         scratch_shapes=[
             pltpu.VMEM((tiles * width, width), f32),
             pltpu.VMEM((cells, 4, width // 8, 8, width), f32),
             pltpu.VMEM((cells, 3 + 5 * types, 8, width), f32),
-            pltpu.VMEM((tiles, width // 8, 8, width), f32),
+            pltpu.VMEM(
+                (len(second_of), sizes[0] * sizes[1] * sizes[2], 3, width // 8, 8, width), f32
+            ),
             pltpu.VMEM((cells, 3, 8, width), f32),
+            pltpu.SMEM((cells,), jnp.int32),
         ],
         compiler_params=pltpu.CompilerParams(vmem_limit_bytes=VMEM_LIMIT),
-    )(ext)
+    )(type_charge, type_sigma, type_epsilon, ext)
     count_x, count_y, count_z = (lax.axis_size(axis) for axis in AXES)
     count_plane = count_y * count_z
     normaliser = 1.0 / (
@@ -430,7 +447,9 @@
             pltpu.SemaphoreType.DMA((count_plane,)),
             pltpu.SemaphoreType.DMA((count_plane,)),
         ],
-        compiler_params=pltpu.CompilerParams(collective_id=1, has_side_effects=True),
+        compiler_params=pltpu.CompilerParams(
+            collective_id=1, has_side_effects=True, vmem_limit_bytes=8 * 1024 * 1024
+        ),
     )(reaction, part)
     return forces, totals
 

time: 107 us -> 53.1 us (0.50)
  Pallas kernels: 80.5 us -> 49.3 us
  other arithmetic: 12.9 us -> 0 us
  local copies, waits for them, and re-layouts: 11 us -> 3.34 us
  between operations: 2 us -> 0.68 us
    pallas_call x1, Pallas kernels: 51.9 us -> 25.6 us  [per_device(): pl.pallas_call(functools.partial(pair_kernel, types), name='pairs', out_s...]
    select_n x2 -> x0, other arithmetic: 10.3 us -> none  [packed_rows(): lines.append(jnp.where(occupied, of_type(values), 0.0))]
    slice x8 -> x0, local copies, waits for them, and re-layouts: 4.33 us -> none  [the longest x4 2.56 us: of_type(): picked = jnp.where(type_ids == kind, values[kind], picked)]
    pallas_call x1, Pallas kernels: 16.7 us -> 14.1 us  [per_device(): pl.pallas_call(functools.partial(return_kernel, normaliser), name='giveba...]
    div x1 -> x0, other arithmetic: 2.56 us -> none  [packed_rows(): (six * cut_sq ** (-3) - twelve * cut_sq ** (-6) - coulomb / cut_len) / cu...]
    pallas_call x1, Pallas kernels: 11.9 us -> 9.62 us  [per_device(): pl.pallas_call(halo_kernel, name='halo', out_shape=jax.ShapeDtypeStruct(e...]
    another operation x2 -> x0, local copies, waits for them, and re-layouts: 1.42 us -> none  [packed_rows(): return jnp.stack(lines, 3)]
    unnamed x17 -> x13, local copies, waits for them, and re-layouts: 4.61 us -> 3.34 us
where the time goes in v2:
time: 53.1 us; the launch traced here: 53.3 us
  Pallas kernels  49.3 us (93%)
  local copies, waits for them, and re-layouts  3.34 us (6%)
  between operations  0.68 us (1%)
    pallas_call x1, Pallas kernels, per_device(): pl.pallas_call(functools.partial(pair_kernel, types), name='pairs', out_s...  25.6 us
    pallas_call x1, Pallas kernels, per_device(): pl.pallas_call(functools.partial(return_kernel, normaliser), name='giveba...  14.1 us
    pallas_call x1, Pallas kernels, per_device(): pl.pallas_call(halo_kernel, name='halo', out_shape=jax.ShapeDtypeStruct(e...  9.62 us
    unnamed x13, local copies, waits for them, and re-layouts  3.34 us

profile of v2, /device:TPU:0, one launch (start us, length us, event | category | flops | bytes accessed | tf_op | source)
XLA Modules:
  0.0 53.3 jit_solution(14306073018261385037)
XLA Ops:
  0.6 0.8 %copy.8.counts = s32[2,4,2]{2,1,0:T(4,128)S(1)} copy(s32[2,4,2]{1,2,0:T(2,128)} %param.8) | data formatting | bytes 128 | tf_op args[2]
  1.4 0.0 copy-start
  1.4 0.7 %copy-done = f32[3,2,4,2,128]{4,3,2,1,0:T(2,128)S(1)} copy-done((f32[3,2,4,2,128]{4,3,2,1,0:T(2,128)S(1)}, f32[3,2,4,2,128]{4,3,2,1,0:T(2,128)}, u32[]{:S(2)}) %copy-start) | copy-done | bytes 24600
  2.1 0.0 copy-start.1
  2.1 0.7 %copy-done.1 = s32[2,4,2,128]{3,2,1,0:T(2,128)S(1)} copy-done((s32[2,4,2,128]{3,2,1,0:T(2,128)S(1)}, s32[2,4,2,128]{3,2,1,0:T(2,128)}, u32[]{:S(2)}) %copy-start.1) | copy-done | bytes 8216
  2.8 0.0 copy-start.2
  2.8 0.0 copy-start.3
  2.8 0.0 copy-start.4
  2.8 9.6 %halo.1.ext = f32[3,5,3,8,128]{4,3,2,1,0:T(8,128)S(1)} custom-call(f32[3,2,4,2,128]{4,3,2,1,0:T(2,128)S(1)} %copy-done, s32[2,4,2,128]{3,2,1,0:T(2,128)S(1)} %copy-done.1, s32[2,4,2]{2,1,0:T(4,128)S(1)} %copy.8.counts), custom_call_target="tpu_custom_call" | custom-call | tf_op jit(solution)/shard_map/halo/pallas_call | solution.py:383
  12.5 0.0 copy-done.2
  12.5 0.0 copy-done.3
  12.5 0.0 copy-done.4
  12.5 25.6 %pairs.1 = (f32[3,5,3,8,128]{4,3,2,1,0:T(8,128)S(1)}, f32[8,128]{1,0:T(8,128)S(1)}) custom-call(f32[2]{0:T(128)S(1)} %copy-done.2, f32[2]{0:T(128)S(1)} %copy-done.3, f32[2]{0:T(128)S(1)} %copy-done.4, f32[3,5,3,8,128]{4,3,2,1,0:T(8,128)S(1)} %halo.1.ext), custom_call_target="tpu_custom_call" | custom-call | tf_op jit(solution)/shard_map/pairs/pallas_call | solution.py:396
  38.1 14.1 %giveback.1 = (f32[3,2,4,2,128]{4,3,2,1,0:T(2,128)S(1)}, f32[2]{0:T(128)S(1)}) custom-call(f32[3,5,3,8,128]{4,3,2,1,0:T(8,128)S(1)} %get-tuple-element.4.reaction, f32[8,128]{1,0:T(8,128)S(1)} %get-tuple-element.5.part), custom_call_target="tpu_custom_call" | custom-call | tf_op jit(solution)/shard_map/giveback/pallas_call | solution.py:429
  52.2 0.6 %copy.11 = f32[3,2,4,2,128]{4,3,2,1,0:T(2,128)} copy(f32[3,2,4,2,128]{4,3,2,1,0:T(2,128)S(1)} %get-tuple-element.8) | data formatting | bytes 49152
  52.8 0.5 copy.12
Async XLA Ops:
  1.4 0.7 %copy-start = (f32[3,2,4,2,128]{4,3,2,1,0:T(2,128)S(1)}, f32[3,2,4,2,128]{4,3,2,1,0:T(2,128)}, u32[]{:S(2)}) copy-start(f32[3,2,4,2,128]{4,3,2,1,0:T(2,128)} %positions.1) | copy-start | bytes 73732
  2.1 0.7 %copy-start.1 = (s32[2,4,2,128]{3,2,1,0:T(2,128)S(1)}, s32[2,4,2,128]{3,2,1,0:T(2,128)}, u32[]{:S(2)}) copy-start(s32[2,4,2,128]{3,2,1,0:T(2,128)} %type_ids.1) | copy-start | bytes 24580
  2.8 9.6 %copy-start.2 = (f32[2]{0:T(128)S(1)}, f32[2]{0:T(128)}, u32[]{:S(2)}) copy-start(f32[2]{0:T(128)} %charges.1) | copy-start | bytes 28
  2.8 9.6 %copy-start.3 = (f32[2]{0:T(128)S(1)}, f32[2]{0:T(128)}, u32[]{:S(2)}) copy-start(f32[2]{0:T(128)} %sigmas.1) | copy-start | bytes 28
  2.8 9.7 %copy-start.4 = (f32[2]{0:T(128)S(1)}, f32[2]{0:T(128)}, u32[]{:S(2)}) copy-start(f32[2]{0:T(128)} %epsilons.1) | copy-start | bytes 28

commit v3 on v2

--- a/solution.py
+++ b/solution.py
@@ -13,6 +13,7 @@
 cut_sq = 1.0 + soft_core
 cut_len = cut_sq**0.5
 second_of = {0: (0, 1, 2, 3, 4, 5, 6, 7), 1: (2, 6), 2: (4, 5), 4: (1, 3)}
+direct_limit = 64
 VMEM_LIMIT = 40 * 1024 * 1024
 
 
@@ -267,7 +268,6 @@
         force = jnp.concatenate(lines, 0)
         reaction[x, y, z, 0:3] = force
         virial = virial - force * rows[pl.ds(4 * cell, 3)]
-    totals[...] = jnp.zeros(totals.shape, jnp.float32)
     totals[0:1] = jnp.sum(energy, 0, keepdims=True)
     totals[1:2] = jnp.sum(virial, 0, keepdims=True)
 
@@ -283,13 +283,20 @@
     at_x, at_y, at_z = (lax.axis_index(axis) for axis in AXES)
     count_plane = count_y * count_z
     at_plane = at_y * count_z + at_z
+    direct = count_x * count_plane <= direct_limit
+    if direct:
+        count_plane, at_plane = count_x * count_plane, at_x * count_plane + at_plane
+        count_x, at_x = 1, 0
 
     def line_target(step):
         return {"gx": lax.rem(at_x + step, count_x)}
 
     def plane_target(step):
         spot = lax.rem(at_plane + step, count_plane)
-        return {"gy": spot // count_z, "gz": lax.rem(spot, count_z)}
+        target = {"gy": lax.rem(spot // count_z, count_y), "gz": lax.rem(spot, count_z)}
+        if direct:
+            target["gx"] = spot // (count_y * count_z)
+        return target
 
     barrier = pltpu.get_barrier_semaphore()
     for which in range(1, 8):
@@ -299,6 +306,21 @@
     for step in range(1, count_plane):
         pl.semaphore_signal(barrier, inc=1, device_id=plane_target(step), device_id_type=MESH)
     pl.semaphore_wait(barrier, 7 + count_x - 1 + count_plane - 1)
+
+    def send_plane():
+        plane_copies = []
+        for step in range(1, count_plane):
+            copy = pltpu.make_async_remote_copy(
+                src_ref=part if direct else middle,
+                dst_ref=plane.at[at_plane],
+                send_sem=plane_send.at[step],
+                recv_sem=plane_recv.at[step],
+                device_id=plane_target(step),
+                device_id_type=MESH,
+            )
+            copy.start()
+            plane_copies.append(copy)
+        return plane_copies
 
     copies = []
     for which in range(1, 8):
@@ -328,14 +350,18 @@
         )
         copy.start()
         line_copies.append(copy)
-    line[at_x] = part[...]
-    for copy in line_copies:
-        copy.wait()
-    summed = line[0]
-    for step in range(1, count_x):
-        summed = summed + line[step]
-    middle[...] = summed
-    plane[at_plane] = summed
+    if not direct:
+        line[at_x] = part[...]
+        for copy in line_copies:
+            copy.wait()
+        summed = line[0]
+        for step in range(1, count_x):
+            summed = summed + line[step]
+        middle[...] = summed
+        plane[at_plane] = summed
+    else:
+        plane_copies = send_plane()
+        plane[at_plane] = part[...]
     for copy in copies:
         copy.wait()
     for x in range(sizes[0]):
@@ -351,18 +377,8 @@
                         ]
                 for axis in range(3):
                     forces[axis, x, y, pl.ds(z, 1)] = value[axis : axis + 1]
-    plane_copies = []
-    for step in range(1, count_plane):
-        copy = pltpu.make_async_remote_copy(
-            src_ref=middle,
-            dst_ref=plane.at[at_plane],
-            send_sem=plane_send.at[step],
-            recv_sem=plane_recv.at[step],
-            device_id=plane_target(step),
-            device_id_type=MESH,
-        )
-        copy.start()
-        plane_copies.append(copy)
+    if not direct:
+        plane_copies = send_plane()
     for copy in plane_copies:
         copy.wait()
     summed = plane[0]
@@ -398,7 +414,7 @@
         name="pairs",
         out_shape=(
             jax.ShapeDtypeStruct(ext_sizes + (8, width), f32),
-            jax.ShapeDtypeStruct((8, width), f32),
+            jax.ShapeDtypeStruct((2, width), f32),
         ),
         in_specs=[smem, smem, smem, vmem],
         out_specs=(vmem, vmem),
@@ -416,6 +432,9 @@
     )(type_charge, type_sigma, type_epsilon, ext)
     count_x, count_y, count_z = (lax.axis_size(axis) for axis in AXES)
     count_plane = count_y * count_z
+    slots_x, slots_plane = count_x, count_plane
+    if count_x * count_plane <= direct_limit:
+        slots_x, slots_plane = 1, count_x * count_plane
     normaliser = 1.0 / (
         sizes[0] * count_x * sizes[1] * count_y * sizes[2] * count_z * width
     )
@@ -439,13 +458,13 @@
         + [
             pltpu.SemaphoreType.DMA((8,)),
             pltpu.SemaphoreType.DMA((8,)),
-            pltpu.VMEM((count_x, 8, width), f32),
-            pltpu.VMEM((count_plane, 8, width), f32),
-            pltpu.VMEM((8, width), f32),
-            pltpu.SemaphoreType.DMA((count_x,)),
-            pltpu.SemaphoreType.DMA((count_x,)),
-            pltpu.SemaphoreType.DMA((count_plane,)),
-            pltpu.SemaphoreType.DMA((count_plane,)),
+            pltpu.VMEM((slots_x, 2, width), f32),
+            pltpu.VMEM((slots_plane, 2, width), f32),
+            pltpu.VMEM((2, width), f32),
+            pltpu.SemaphoreType.DMA((slots_x,)),
+            pltpu.SemaphoreType.DMA((slots_x,)),
+            pltpu.SemaphoreType.DMA((slots_plane,)),
+            pltpu.SemaphoreType.DMA((slots_plane,)),
         ],
         compiler_params=pltpu.CompilerParams(
             collective_id=1, has_side_effects=True, vmem_limit_bytes=8 * 1024 * 1024

time: 53.1 us -> 51.8 us (0.976); the launches traced: 53.3 us -> 51.1 us
  Pallas kernels: 49.3 us -> 47 us
    pallas_call x1, Pallas kernels: 14.1 us -> 10.7 us  [per_device(): pl.pallas_call(functools.partial(return_kernel, normaliser), name='giveba...]
    pallas_call x1, Pallas kernels: 25.6 us -> 26.7 us  [per_device(): pl.pallas_call(functools.partial(pair_kernel, types), name='pairs', out_s...]
where the time goes in v3:
time: 51.8 us; the launch traced here: 51.1 us
  Pallas kernels  47 us (91%)
  local copies, waits for them, and re-layouts  3.34 us (6%)
  between operations  0.68 us (1%)
    pallas_call x1, Pallas kernels, per_device(): pl.pallas_call(functools.partial(pair_kernel, types), name='pairs', out_s...  26.7 us
    pallas_call x1, Pallas kernels, per_device(): pl.pallas_call(functools.partial(return_kernel, normaliser), name='giveba...  10.7 us
    pallas_call x1, Pallas kernels, per_device(): pl.pallas_call(halo_kernel, name='halo', out_shape=jax.ShapeDtypeStruct(e...  9.62 us
    unnamed x13, local copies, waits for them, and re-layouts  3.34 us

profile of v3, /device:TPU:0, one launch (start us, length us, event | category | flops | bytes accessed | tf_op | source)
XLA Modules:
  0.0 51.1 jit_solution(2707478176668031865)
XLA Ops:
  0.6 0.8 %copy.8.counts = s32[2,4,2]{2,1,0:T(4,128)S(1)} copy(s32[2,4,2]{1,2,0:T(2,128)} %param.8) | data formatting | bytes 128 | tf_op args[2]
  1.4 0.0 copy-start
  1.4 0.7 %copy-done = f32[3,2,4,2,128]{4,3,2,1,0:T(2,128)S(1)} copy-done((f32[3,2,4,2,128]{4,3,2,1,0:T(2,128)S(1)}, f32[3,2,4,2,128]{4,3,2,1,0:T(2,128)}, u32[]{:S(2)}) %copy-start) | copy-done | bytes 24600
  2.1 0.0 copy-start.1
  2.1 0.7 %copy-done.1 = s32[2,4,2,128]{3,2,1,0:T(2,128)S(1)} copy-done((s32[2,4,2,128]{3,2,1,0:T(2,128)S(1)}, s32[2,4,2,128]{3,2,1,0:T(2,128)}, u32[]{:S(2)}) %copy-start.1) | copy-done | bytes 8216
  2.8 0.0 copy-start.2
  2.8 0.0 copy-start.3
  2.8 0.0 copy-start.4
  2.8 9.6 %halo.1.ext = f32[3,5,3,8,128]{4,3,2,1,0:T(8,128)S(1)} custom-call(f32[3,2,4,2,128]{4,3,2,1,0:T(2,128)S(1)} %copy-done, s32[2,4,2,128]{3,2,1,0:T(2,128)S(1)} %copy-done.1, s32[2,4,2]{2,1,0:T(4,128)S(1)} %copy.8.counts), custom_call_target="tpu_custom_call" | custom-call | tf_op jit(solution)/shard_map/halo/pallas_call | solution.py:399
  12.5 0.0 copy-done.2
  12.5 0.0 copy-done.3
  12.5 0.0 copy-done.4
  12.5 26.7 %pairs.1 = (f32[3,5,3,8,128]{4,3,2,1,0:T(8,128)S(1)}, f32[2,128]{1,0:T(2,128)S(1)}) custom-call(f32[2]{0:T(128)S(1)} %copy-done.2, f32[2]{0:T(128)S(1)} %copy-done.3, f32[2]{0:T(128)S(1)} %copy-done.4, f32[3,5,3,8,128]{4,3,2,1,0:T(8,128)S(1)} %halo.1.ext), custom_call_target="tpu_custom_call" | custom-call | tf_op jit(solution)/shard_map/pairs/pallas_call | solution.py:412
  39.2 10.7 %giveback.1 = (f32[3,2,4,2,128]{4,3,2,1,0:T(2,128)S(1)}, f32[2]{0:T(128)S(1)}) custom-call(f32[3,5,3,8,128]{4,3,2,1,0:T(8,128)S(1)} %get-tuple-element.4.reaction, f32[2,128]{1,0:T(2,128)S(1)} %get-tuple-element.5.part), custom_call_target="tpu_custom_call" | custom-call | tf_op jit(solution)/shard_map/giveback/pallas_call | solution.py:448
  49.9 0.6 %copy.11 = f32[3,2,4,2,128]{4,3,2,1,0:T(2,128)} copy(f32[3,2,4,2,128]{4,3,2,1,0:T(2,128)S(1)} %get-tuple-element.8) | data formatting | bytes 49152
  50.5 0.5 %copy.12 = f32[2]{0:T(128)} copy(f32[2]{0:T(128)S(1)} %get-tuple-element.9) | data formatting | bytes 16
Async XLA Ops:
  1.4 0.7 %copy-start = (f32[3,2,4,2,128]{4,3,2,1,0:T(2,128)S(1)}, f32[3,2,4,2,128]{4,3,2,1,0:T(2,128)}, u32[]{:S(2)}) copy-start(f32[3,2,4,2,128]{4,3,2,1,0:T(2,128)} %positions.1) | copy-start | bytes 73732
  2.1 0.7 %copy-start.1 = (s32[2,4,2,128]{3,2,1,0:T(2,128)S(1)}, s32[2,4,2,128]{3,2,1,0:T(2,128)}, u32[]{:S(2)}) copy-start(s32[2,4,2,128]{3,2,1,0:T(2,128)} %type_ids.1) | copy-start | bytes 24580
  2.8 9.6 %copy-start.2 = (f32[2]{0:T(128)S(1)}, f32[2]{0:T(128)}, u32[]{:S(2)}) copy-start(f32[2]{0:T(128)} %charges.1) | copy-start | bytes 28
  2.8 9.6 %copy-start.3 = (f32[2]{0:T(128)S(1)}, f32[2]{0:T(128)}, u32[]{:S(2)}) copy-start(f32[2]{0:T(128)} %sigmas.1) | copy-start | bytes 28
  2.8 9.7 %copy-start.4 = (f32[2]{0:T(128)S(1)}, f32[2]{0:T(128)}, u32[]{:S(2)}) copy-start(f32[2]{0:T(128)} %epsilons.1) | copy-start | bytes 28
